TPU v7x, 32 devices: a whole 2x2x4 slice. The times are simulated.
32 devices in a mesh: rep: 1, dp: 32 (over x, y, z, core).
Axes of the slice: x: 2, y: 2, z: 4, core: 2. Of those that a mesh axis runs over, the one named last changes fastest.
Arguments:
- x: bfloat16 [32, 2048, 768], P(('rep', 'dp'))
- dy: bfloat16 [32, 2048, 768], P(('rep', 'dp'))
- w_gate: bfloat16 [2, 768, 3072], replicated
- w_up: bfloat16 [2, 768, 3072], replicated
- w_down: bfloat16 [2, 3072, 768], replicated
- m_w_gate: float32 [2, 768, 3072], replicated
- m_w_up: float32 [2, 768, 3072], replicated
- m_w_down: float32 [2, 3072, 768], replicated
- v_w_gate: float32 [2, 768, 3072], replicated
- v_w_up: float32 [2, 768, 3072], replicated
- v_w_down: float32 [2, 3072, 768], replicated
Outputs:
- output 1: bfloat16 [2, 768, 3072], P('rep')
- output 2: bfloat16 [2, 768, 3072], P('rep')
- output 3: bfloat16 [2, 3072, 768], P('rep')
- output 4: float32 [2, 768, 3072], P('rep')
- output 5: float32 [2, 768, 3072], P('rep')
- output 6: float32 [2, 3072, 768], P('rep')
- output 7: float32 [2, 768, 3072], P('rep')
- output 8: float32 [2, 768, 3072], P('rep')
- output 9: float32 [2, 3072, 768], P('rep')
All inputs are finite; a program needn't handle non-finite values.
Results may differ from a plain program's by a relative error of at most 0.022.
Values are sent between devices in bfloat16 or wider.
A program may use at most 2.5 GiB of HBM per device.

v0:
```python
import jax
import jax.numpy as jnp
from jax import lax
from jax.sharding import PartitionSpec as P

NAMES = ("w_gate", "w_up", "w_down")


def matmul(a, w):
    return jnp.dot(a, w, preferred_element_type=jnp.float32).astype(jnp.bfloat16)


def normed(h):
    wide = h.astype(jnp.float32)
    scale = lax.rsqrt(jnp.mean(wide**2, -1, keepdims=True) + 1e-6)
    return (wide * scale).astype(jnp.bfloat16)


def layer(h, w):
    a = normed(h)
    gate = jnp.dot(a, w["w_gate"], preferred_element_type=jnp.float32)
    up = jnp.dot(a, w["w_up"], preferred_element_type=jnp.float32)
    return h + matmul((jax.nn.silu(gate) * up).astype(jnp.bfloat16), w["w_down"])


def adamw(w, m, v, g):
    m = 0.9 * m + 0.1 * g
    v = 0.95 * v + 0.05 * g * g
    step = m * lax.rsqrt(v + 1e-8) + 0.1 * w
    return (w - 0.02 * step).astype(jnp.bfloat16), m, v


def clipped(gradients, sum_of_squares, count):
    factor = jnp.minimum(1.0, 0.5 * lax.rsqrt(sum_of_squares / count + 1e-30))
    return [g * factor for g in gradients]


def solution(mesh):
    def step(x, dy, *arrays):
        weights, m, v = (arrays[i : i + 3] for i in (0, 3, 6))
        layers = weights[0].shape[0]
        h, kept = x[0], []
        for number in range(layers):
            kept.append(h)
            h = layer(h, {name: w[number] for name, w in zip(NAMES, weights, strict=True)})
        by_h, summed = dy[0], [None] * layers
        for number in reversed(range(layers)):
            _, back = jax.vjp(lambda w, h: layer(h, w), {name: w[number] for name, w in zip(NAMES, weights, strict=True)}, kept[number])
            by_w, by_h = back(by_h)
            summed[number] = [lax.psum(by_w[name], "dp") for name in NAMES]
        gradients = [jnp.stack([summed[number][i] for number in range(layers)]).astype(jnp.float32) for i in range(3)]
        gradients = clipped(gradients, sum(jnp.sum(g * g) for g in gradients), sum(g.size for g in gradients))
        new = [adamw(w.astype(jnp.float32), m, v, g) for w, m, v, g in zip(weights, m, v, gradients, strict=True)]
        return tuple(one[which] for which in range(3) for one in new)

    return jax.shard_map(
        step,
        mesh=mesh,
        in_specs=(P(("rep", "dp"), None, None),) * 2 + (P(None, None, None),) * 9,
        out_specs=(P("rep", None, None),) * 9,
        check_vma=False,
    )
```

profile of v0, /device:TPU:0, one launch (start us, length us, event | category | flops | bytes accessed | tf_op | source)
XLA Modules:
  0.0 889.8 jit_solution(14349736251065481932)
XLA Ops:
  7.2 3.2 copy.20
  11.1 5.0 copy.21
  16.1 15.8 %convolution_convert_fusion.1 = bf16[2048,3072]{1,0:T(8,128)(2,1)} fusion(bf16[2,3072,768]{2,1,0:T(8,128)(2,1)} %param.15, bf16[1,2048,768]{2,1,0:T(8,128)(2,1)} %param.12), kind=kOutput, calls=%fused_computation.61 | convolution fusion | flops 9669967872 | bytes 20447232 | tf_op jit(solution)/shard_map/transpose(jvp())/dot_general | solution.py:10
  32.0 15.9 %fusion.62 = f32[2048,3072]{1,0:T(8,128)} fusion(bf16[2,768,3072]{2,1,0:T(8,128)(2,1)} %param.13, bf16[1,2048,768]{2,1,0:T(8,128)(2,1)S(1)} %copy-done.4, f32[2048]{0:T(1024)S(1)} %add_rsqrt_fusion), kind=kOutput, calls=%fused_computation.99 | convolution fusion | flops 9668395008 | bytes 33038336 | tf_op jit(solution)/shard_map/dot_general | solution.py:21
  47.9 27.8 %multiply_convert_fusion.1 = (bf16[2048,3072]{1,0:T(8,128)(2,1)}, f32[2048,3072]{1,0:T(8,128)}) fusion(f32[2048,3072]{1,0:T(8,128)} %fusion.62, bf16[2,768,3072]{2,1,0:T(8,128)(2,1)} %param.14, bf16[1,2048,768]{2,1,0:T(8,128)(2,1)} %param.11, f32[2048]{0:T(1024)S(1)} %add_rsqrt_fusion), kind=kOutput, calls=%fused_computation.20 | convolution fusion | flops 9706143744 | bytes 70787072 | tf_op jit(solution)/shard_map/dot_general | solution.py:22
  75.7 15.1 %fusion.40 = (f32[2048]{0:T(1024)S(1)}, bf16[2048,768]{0,1:T(8,128)(2,1)S(1)}) fusion(bf16[2048,3072]{1,0:T(8,128)(2,1)} %get-tuple-element.24, bf16[2,3072,768]{2,1,0:T(8,128)(2,1)} %param.15, bf16[1,2048,768]{1,2,0:T(8,128)(2,1)S(1)} %copy.20), kind=kOutput, calls=%fused_computation.76 | convolution fusion | flops 9671538688 | bytes 23601152 | tf_op jit(solution)/shard_map/dot_general | solution.py:10
  92.4 15.7 %fusion.49 = f32[2048,3072]{1,0:T(8,128)} fusion(bf16[2,768,3072]{2,1,0:T(8,128)(2,1)} %param.14, bf16[2048,768]{0,1:T(8,128)(2,1)S(1)} %get-tuple-element.27, f32[2048]{0:T(1024)S(1)} %fusion.108), kind=kOutput, calls=%fused_computation.86 | convolution fusion | flops 9668395008 | bytes 33038336 | tf_op jit(solution)/shard_map/jvp()/dot_general | solution.py:22
  108.1 39.7 %fusion.2 = (bf16[2048,3072]{1,0:T(8,128)(2,1)}, f32[2048,3072]{1,0:T(8,128)}) fusion(f32[2048,3072]{1,0:T(8,128)} %fusion.49, bf16[2048,3072]{1,0:T(8,128)(2,1)} %convolution_convert_fusion.1, bf16[2,768,3072]{2,1,0:T(8,128)(2,1)} %param.13, bf16[2048,768]{0,1:T(8,128)(2,1)} %copy-done.6, f32[2048]{0:T(1024)S(1)} %fusion.108), kind=kOutput, calls=%fused_computation.11 | convolution fusion | flops 9743892480 | bytes 83369984 | tf_op jit(solution)/shard_map/jvp()/dot_general | solution.py:21
  147.8 18.6 %fusion.82 = bf16[2048,768]{0,1:T(8,128)(2,1)} fusion(bf16[2,768,3072]{2,1,0:T(8,128)(2,1)} %param.14, bf16[2048,3072]{1,0:T(8,128)(2,1)} %convolution_convert_fusion.1, f32[2048,3072]{1,0:T(8,128)} %get-tuple-element.29), kind=kOutput, calls=%fused_computation.116 | convolution fusion | flops 9702998016 | bytes 45613056 | tf_op jit(solution)/shard_map/transpose(jvp())/dot_general | solution.py:22
  166.4 19.6 %fusion.74 = bf16[1,768,3072]{2,1,0:T(8,128)(2,1)} fusion(bf16[2048,3072]{1,0:T(8,128)(2,1)} %convolution_convert_fusion.1, bf16[2048,768]{0,1:T(8,128)(2,1)} %copy-done.6, f32[2048]{0:T(1024)S(1)} %fusion.108, f32[2048,3072]{1,0:T(8,128)} %get-tuple-element.29), kind=kOutput, calls=%fused_computation.109 | convolution fusion | flops 9708503040 | bytes 45621248 | tf_op jit(solution)/shard_map/transpose(jvp())/dot_general | solution.py:22
  186.1 22.4 %fusion.71 = bf16[1,3072,768]{2,1,0:T(8,128)(2,1)} fusion(f32[2048,3072]{1,0:T(8,128)} %fusion.49, bf16[1,2048,768]{2,1,0:T(8,128)(2,1)S(1)} %copy-done.5, f32[2048,3072]{1,0:T(8,128)} %get-tuple-element.29), kind=kOutput, calls=%fused_computation.106 | convolution fusion | flops 9703784448 | bytes 58195968 | tf_op jit(solution)/shard_map/transpose(jvp())/dot_general | solution.py:10
  208.4 17.4 %fusion.70 = bf16[1,768,3072]{2,1,0:T(8,128)(2,1)} fusion(bf16[2048,3072]{1,0:T(8,128)(2,1)} %get-tuple-element.28, bf16[2048,768]{0,1:T(8,128)(2,1)} %copy-done.6, f32[2048]{0:T(1024)S(1)} %fusion.108), kind=kOutput, calls=%fused_computation.105 | convolution fusion | flops 9668395008 | bytes 20455424 | tf_op jit(solution)/shard_map/transpose(jvp())/dot_general | solution.py:21
  225.8 16.4 %fusion.42 = (f32[2048]{0:T(1024)S(1)}, bf16[2048,768]{0,1:T(8,128)(2,1)}) fusion(bf16[2048,768]{0,1:T(8,128)(2,1)S(1)} %copy-done.7, bf16[2048,768]{0,1:T(8,128)(2,1)} %fusion.82, bf16[2048,3072]{1,0:T(8,128)(2,1)} %get-tuple-element.28, bf16[2,768,3072]{2,1,0:T(8,128)(2,1)} %param.13), kind=kOutput, calls=%fused_computation.78 | convolution fusion | flops 9671538688 | bytes 26746880 | tf_op jit(solution)/shard_map/transpose(jvp())/dot_general | solution.py:21
  242.2 5.8 fusion.92
  248.0 14.6 %convolution_convert_fusion = bf16[2048,3072]{1,0:T(8,128)(2,1)} fusion(bf16[2048,768]{0,1:T(8,128)(2,1)} %fusion.92, bf16[2,3072,768]{2,1,0:T(8,128)(2,1)S(1)} %bitcast.85), kind=kOutput, calls=%fused_computation.60 | convolution fusion | flops 9669967872 | bytes 20447232 | tf_op jit(solution)/shard_map/transpose(jvp())/dot_general | solution.py:10
  262.6 15.6 %fusion.72 = bf16[1,3072,768]{2,1,0:T(8,128)(2,1)} fusion(bf16[2048,3072]{1,0:T(8,128)(2,1)} %get-tuple-element.24, bf16[2048,768]{0,1:T(8,128)(2,1)} %fusion.92), kind=kOutput, calls=%fused_computation.107 | convolution fusion | flops 9666035712 | bytes 20447232 | tf_op jit(solution)/shard_map/transpose(jvp())/dot_general | solution.py:10
  278.2 18.6 %fusion.73 = bf16[1,768,3072]{2,1,0:T(8,128)(2,1)} fusion(bf16[2048,3072]{1,0:T(8,128)(2,1)} %convolution_convert_fusion, f32[2048,3072]{1,0:T(8,128)} %fusion.62, bf16[1,2048,768]{1,2,0:T(8,128)(2,1)S(1)} %copy-done.2, f32[2048]{0:T(1024)S(1)} %copy-done.11), kind=kOutput, calls=%fused_computation.108 | convolution fusion | flops 9708503040 | bytes 45621248 | tf_op jit(solution)/shard_map/transpose(jvp())/dot_general | solution.py:22
  296.8 26.0 %fusion.67 = bf16[1,768,3072]{2,1,0:T(8,128)(2,1)} fusion(f32[2048,3072]{1,0:T(8,128)} %fusion.62, f32[2048,3072]{1,0:T(8,128)} %get-tuple-element.25, bf16[2048,3072]{1,0:T(8,128)(2,1)} %convolution_convert_fusion, bf16[1,2048,768]{1,2,0:T(8,128)(2,1)S(1)} %copy-done.2, f32[2048]{0:T(1024)S(1)} %copy-done.11), kind=kOutput, calls=%fused_computation.104 | convolution fusion | flops 9739960320 | bytes 70787072 | tf_op jit(solution)/shard_map/transpose(jvp())/dot_general | solution.py:21
  322.8 433.0 %all-reduce.3.cloned.1.call-done = (bf16[1,768,3072]{2,1,0:T(8,128)(2,1)}, bf16[1,768,3072]{2,1,0:T(8,128)(2,1)}, bf16[1,768,3072]{2,1,0:T(8,128)(2,1)}, bf16[1,...) async-done(((bf16[1,768,3072]{2,1,0:T(8,128)(2,1)}, bf16[1,768,3072]{2,1,0:T(8,128)(2,1)}, bf16[1,768,3072]{2,1,0:T(8,128)(2,1)}, ...) | async-done | bytes 28311568 | tf_op jit(solution)/shard_map/psum | solution.py:50
  755.9 9.4 %fusion.20 = f32[]{:T(128)} fusion(bf16[1,768,3072]{2,1,0:T(8,128)(2,1)} %get-tuple-element.9, bf16[1,768,3072]{2,1,0:T(8,128)(2,1)} %get-tuple-element.10), kind=kLoop, calls=%fused_computation.44 | loop fusion | flops 18874368 | bytes 9437188 | tf_op jit(solution)/shard_map/reduce_sum | solution.py:52
  765.2 5.5 fusion.21
  772.0 9.3 %fusion.22 = f32[]{:T(128)} fusion(bf16[1,3072,768]{2,1,0:T(8,128)(2,1)} %get-tuple-element.13, bf16[1,3072,768]{2,1,0:T(8,128)(2,1)} %get-tuple-element.14), kind=kLoop, calls=%fused_computation.46 | loop fusion | flops 18874368 | bytes 9437188 | tf_op jit(solution)/shard_map/reduce_sum | solution.py:52
  782.0 37.1 %fusion.28 = (bf16[2,3072,768]{2,1,0:T(8,128)(2,1)}, f32[2,3072,768]{2,1,0:T(8,128)}, f32[2,3072,768]{2,1,0:T(8,128)}) fusion(bf16[2,3072,768]{2,1,0:T(8,128)(2,1)} %param.15, f32[]{:T(128)S(6)} %min_shard_map.3, bf16[1,3072,768]{2,1,0:T(8,128)(2,1)} %get-tuple-element.13, bf16[1,3072,768]{2,1,0:T(8,128)(2,1)} %get-tuple-element.14, ...), kind=kLoop, calls=%fused_computation.52 | loop fusion | flops 94371840 | bytes 103809024 | tf_op jit(solution)/shard_map/convert_element_type | solution.py:30
  819.1 63.3 %fusion.19 = (bf16[2,768,3072]{2,1,0:T(8,128)(2,1)}, f32[2,768,3072]{2,1,0:T(8,128)}, f32[2,768,3072]{2,1,0:T(8,128)}, bf16[2,768,3072]{2,1,0:T(8,128)(2,1)}, f3...) fusion(bf16[2,768,3072]{2,1,0:T(8,128)(2,1)} %param.13, f32[]{:T(128)S(6)} %min_shard_map.3, ...), kind=kLoop, calls=%fused_computation.43 | loop fusion | flops 188743680 | bytes 207618048 | tf_op jit(solution)/shard_map/convert_element_type | solution.py:30
  (47 shorter events, 2.5 us)
Async XLA Ops:
  7.2 748.7 %all-reduce.3.cloned.1.call-start = ((), (), s32[]{:S(2)}) async-start(), calls=%async_computation | async-start | bytes 56623104 | tf_op jit(solution)/shard_map/psum | solution.py:50
  10.4 65.3 %copy-start.1 = (bf16[1,2048,768]{1,2,0:T(8,128)(2,1)}, bf16[1,2048,768]{1,2,0:T(8,128)(2,1)S(1)}, u32[]{:S(2)}) copy-start(bf16[1,2048,768]{1,2,0:T(8,128)(2,1)S(1)} %copy.20) | copy-start | bytes 9437188
  11.1 36.8 %copy-start.10 = (f32[2048]{0:T(1024)}, f32[2048]{0:T(1024)S(1)}, u32[]{:S(2)}) copy-start(f32[2048]{0:T(1024)S(1)} %add_rsqrt_fusion) | copy-start | bytes 24580
  16.1 15.8 %copy-start.4 = (bf16[1,2048,768]{2,1,0:T(8,128)(2,1)S(1)}, bf16[1,2048,768]{2,1,0:T(8,128)(2,1)}, u32[]{:S(2)}) copy-start(bf16[1,2048,768]{2,1,0:T(8,128)(2,1)} %param.11) | copy-start | bytes 9437188
  90.7 0.6 copy-start.8
  90.8 1.7 copy-start.6
  166.4 19.7 %copy-start.5 = (bf16[1,2048,768]{2,1,0:T(8,128)(2,1)S(1)}, bf16[1,2048,768]{2,1,0:T(8,128)(2,1)}, u32[]{:S(2)}) copy-start(bf16[1,2048,768]{2,1,0:T(8,128)(2,1)} %param.12) | copy-start | bytes 9437188
  208.4 17.4 %copy-start.7 = (bf16[2048,768]{0,1:T(8,128)(2,1)S(1)}, bf16[2048,768]{0,1:T(8,128)(2,1)}, u32[]{:S(2)}) copy-start(bf16[2048,768]{0,1:T(8,128)(2,1)} %copy-done.6) | copy-start | bytes 9437188
  208.4 39.6 %slice-start.4 = ((s8[9437184]{0:T(1024)(128)(4,1)}), s8[4194304]{0:T(1024)(128)(4,1)S(1)}, s32[]{:S(2)}) async-start(s8[9437184]{0:T(1024)(128)(4,1)} %bitcast.84), calls=%async_computation.5 | async-start | bytes 8388608
  208.4 39.6 %slice-start.5 = ((s8[9437184]{0:T(1024)(128)(4,1)}), s8[4194304]{0:T(1024)(128)(4,1)S(1)}, s32[]{:S(2)}) async-start(s8[9437184]{0:T(1024)(128)(4,1)} %bitcast.84), calls=%async_computation.6 | async-start | bytes 8388608
  225.8 16.4 %copy-start.9 = (f32[2048]{0:T(1024)S(1)}, f32[2048]{0:T(1024)}, u32[]{:S(2)}) copy-start(f32[2048]{0:T(1024)} %copy-done.8) | copy-start | bytes 24580
  225.8 16.4 %copy-start.3 = (bf16[1,2048,768]{1,2,0:T(8,128)(2,1)S(1)}, bf16[1,2048,768]{1,2,0:T(8,128)(2,1)}, u32[]{:S(2)}) copy-start(bf16[1,2048,768]{1,2,0:T(8,128)(2,1)} %copy.21) | copy-start | bytes 9437188
  225.8 22.2 %slice-start.6 = ((s8[9437184]{0:T(1024)(128)(4,1)}), s8[1048576]{0:T(1024)(128)(4,1)S(1)}, s32[]{:S(2)}) async-start(s8[9437184]{0:T(1024)(128)(4,1)} %bitcast.84), calls=%async_computation.7 | async-start | bytes 2097152
  262.6 15.6 %copy-start.2 = (bf16[1,2048,768]{1,2,0:T(8,128)(2,1)S(1)}, bf16[1,2048,768]{1,2,0:T(8,128)(2,1)}, u32[]{:S(2)}) copy-start(bf16[1,2048,768]{1,2,0:T(8,128)(2,1)} %copy-done.1) | copy-start | bytes 9437188
  262.6 15.6 %copy-start.11 = (f32[2048]{0:T(1024)S(1)}, f32[2048]{0:T(1024)}, u32[]{:S(2)}) copy-start(f32[2048]{0:T(1024)} %copy-done.10) | copy-start | bytes 24580
  755.9 9.4 %slice-start.2 = ((s8[4718592]{0:T(1024)(128)(4,1)}), s8[4194304]{0:T(1024)(128)(4,1)S(1)}, s32[]{:S(2)}) async-start(s8[4718592]{0:T(1024)(128)(4,1)} %bitcast.82), calls=%async_computation.3 | async-start | bytes 8388608
  755.9 9.4 %copy-start = (bf16[1,768,3072]{2,1,0:T(8,128)(2,1)S(1)}, bf16[1,768,3072]{2,1,0:T(8,128)(2,1)}, u32[]{:S(2)}) copy-start(bf16[1,768,3072]{2,1,0:T(8,128)(2,1)} %get-tuple-element.12) | copy-start | bytes 14155780
  755.9 9.4 %slice-start.3 = ((s8[4718592]{0:T(1024)(128)(4,1)}), s8[524288]{0:T(1024)(128)(4,1)S(1)}, s32[]{:S(2)}) async-start(s8[4718592]{0:T(1024)(128)(4,1)} %bitcast.82), calls=%async_computation.4 | async-start | bytes 1048576
  772.0 47.1 %slice-start = ((s8[4718592]{0:T(1024)(128)(4,1)}), s8[524288]{0:T(1024)(128)(4,1)S(1)}, s32[]{:S(2)}) async-start(s8[4718592]{0:T(1024)(128)(4,1)} %bitcast.80), calls=%async_computation.1 | async-start | bytes 1048576
  782.0 37.2 %slice-start.1 = ((s8[4718592]{0:T(1024)(128)(4,1)}), s8[4194304]{0:T(1024)(128)(4,1)S(1)}, s32[]{:S(2)}) async-start(s8[4718592]{0:T(1024)(128)(4,1)} %bitcast.80), calls=%async_computation.2 | async-start | bytes 8388608
Sparse Core Ops, SparseCore 0:
  322.9 432.8 all-reduce.2
where the time goes:
time: 897 us; the launch traced here: 890 us
  waiting for transfers between devices  433 us (48%)
  matrix products  299 us (33%)
  other arithmetic  131 us (15%)
  between operations  16.7 us (2%)
  local copies, waits for them, and re-layouts  9.95 us (1%)
    psum x1, waiting for transfers between devices, step(): summed[number] = [lax.psum(by_w[name], 'dp') for name in NAMES]  433 us
    dot_general x5, matrix products, layer(): gate = jnp.dot(a, w['w_gate'], preferred_element_type=jnp.float32)  115 us
    convert_element_type x2, other arithmetic, adamw(): return ((w - 0.02 * step).astype(jnp.bfloat16), m, v)  100 us
    dot_general x5, matrix products, layer(): up = jnp.dot(a, w['w_up'], preferred_element_type=jnp.float32)  100 us
    dot_general x5, matrix products, matmul(): jnp.dot(a, w, preferred_element_type=jnp.float32).astype(jnp.bfloat16)  83.4 us
    reduce_sum x3, other arithmetic, step(): jnp.sum(g * g)  24.1 us
  transfers between devices with their start and end apart: 1, of which 1 were waited for; matrix products, arithmetic and copies ran while one was open for 0% of the time, Pallas kernels for 0%

commit v1 on v0

v1 whole, which is shorter than its diff:
```python
import functools

import jax
import jax.numpy as jnp
from jax import lax
from jax.experimental import pallas as pl
from jax.experimental.pallas import tpu as pltpu
from jax.sharding import PartitionSpec as P

D, FF = 768, 3072
MESH = pl.DeviceIdType.MESH
HALF, COLOR, FIRST, SECOND = 384, 192, 96, 48
ZS = 4
WIDE, TALL = 512, 192
VMEM_LIMIT = 63 * 1024 * 1024
F32, BF16 = jnp.float32, jnp.bfloat16


OPT_STEPS = 12


def adamw_kernel(count, square_ref, *refs):
    factor = jnp.minimum(1.0, 0.5 * lax.rsqrt(jnp.sum(square_ref[...], keepdims=True) / count + 1e-30))
    for k in range(3):
        w, m, v, g, new_w, new_m, new_v = (refs[k + 3 * i] for i in range(7))

        @pl.when(pl.program_id(0) // OPT_STEPS == k)
        def _():
            rows = 128 if k == 2 else 16

            def body(r, _):
                at = pl.ds(pl.multiple_of(r * rows, rows), rows)
                wide = (g[:, at].astype(F32).T if k == 2 else g[at].astype(F32)) * factor
                mm = 0.9 * m[at] + 0.1 * wide
                vv = 0.95 * v[at] + 0.05 * wide * wide
                ww = w[at].astype(F32)
                new_m[at], new_v[at] = mm, vv
                new_w[at] = (ww - 0.02 * (mm * lax.rsqrt(vv + 1e-8) + 0.1 * ww)).astype(BF16)
                return 0

            lax.fori_loop(0, w.shape[0] // rows, body, 0)


def adamw(square, *arrays):
    def spec(k):
        if k == 11:
            turns, step = OPT_STEPS // 2, lambda t: jnp.clip(t - 2 * OPT_STEPS, 0, OPT_STEPS - 1)
            return pl.BlockSpec((D, FF // turns), lambda t: (step(t) // turns, step(t) % turns))
        rows, columns = arrays[k % 3].shape
        return pl.BlockSpec((rows // OPT_STEPS, columns), lambda t: (jnp.clip(t - OPT_STEPS * (k % 3), 0, OPT_STEPS - 1), 0))

    specs = [spec(k) for k in range(12)]
    like = lambda k, dtype: jax.ShapeDtypeStruct(arrays[k].shape, dtype)
    return pl.pallas_call(
        functools.partial(adamw_kernel, sum(w.size for w in arrays[:3])),
        grid=(3 * OPT_STEPS,),
        in_specs=[pl.BlockSpec((8, 128), lambda t: (0, 0))] + specs,
        out_specs=specs[:9],
        out_shape=[like(k, BF16) for k in range(3)] + [like(k, F32) for k in range(3)] * 2,
        compiler_params=pltpu.CompilerParams(dimension_semantics=("arbitrary",), vmem_limit_bytes=VMEM_LIMIT),
        name="adamw",
    )(square, *arrays)


TT, FC = 256, 768


def dot(a, b, dims=((1,), (0,))):
    return lax.dot_general(a, b, (dims, ((), ())), preferred_element_type=F32)


def rms_scale(wide):
    return lax.rsqrt(jnp.mean(wide * wide, -1, keepdims=True) + 1e-6)


def tokens_kernel(x_ref, dy_ref, wg_hbm, wu_hbm, wd_hbm, a0_ref, a1_ref, dy_out, dh_ref, act0, dg0, du0, act1, dg1, du1, wg, wu, wd, keep_g, keep_u, sem):
    step = pl.program_id(0)
    loads = [
        pltpu.make_async_copy(hbm.at[l], vmem.at[l], sem.at[l * 3 + k])
        for l in range(2)
        for k, (hbm, vmem) in enumerate(((wg_hbm, wg), (wu_hbm, wu), (wd_hbm, wd)))
    ]

    @pl.when(step == 0)
    def _():
        for load in loads:
            load.start()

    def ready(*which):
        @pl.when(step == 0)
        def _():
            for k in which:
                loads[k].wait()

    h0 = x_ref[...].astype(F32)
    a0 = (h0 * rms_scale(h0)).astype(BF16)
    a0_ref[...] = a0.T
    ready(0, 1, 2)
    total = jnp.zeros((TT, D), F32)
    for j in range(FF // FC):
        at = slice(j * FC, (j + 1) * FC)
        gate, up = dot(a0, wg[0, :, at]), dot(a0, wu[0, :, at])
        keep_g[:, at], keep_u[:, at] = gate, up
        act = (gate * jax.nn.sigmoid(gate) * up).astype(BF16)
        act0[:, at] = act
        total = total + dot(act, wd[0, at, :])
    h1 = (h0 + total.astype(BF16).astype(F32)).astype(BF16).astype(F32)
    scale1 = rms_scale(h1)
    a1 = (h1 * scale1).astype(BF16)
    a1_ref[...] = a1.T
    ready(3, 4, 5)

    def back(dact, gate, up):
        dact = dact.astype(BF16).astype(F32)
        sig = jax.nn.sigmoid(gate)
        silu = gate * sig
        return silu * up, dact * up * (sig + silu * (1.0 - sig)), dact * silu

    dy = dy_ref[...]
    dy_out[...] = dy.T
    by_gate, by_up = jnp.zeros((TT, D), F32), jnp.zeros((TT, D), F32)
    nt = ((1,), (1,))
    for j in range(FF // FC):
        at = slice(j * FC, (j + 1) * FC)
        gate, up = dot(a1, wg[1, :, at]), dot(a1, wu[1, :, at])
        act, dg, du = back(dot(dy, wd[1, at, :], nt), gate, up)
        dg, du = dg.astype(BF16), du.astype(BF16)
        act1[:, at], dg1[:, at], du1[:, at] = act.astype(BF16), dg, du
        by_gate = by_gate + dot(dg, wg[1, :, at], nt)
        by_up = by_up + dot(du, wu[1, :, at], nt)
    da = (by_gate.astype(BF16).astype(F32) + by_up.astype(BF16).astype(F32)).astype(BF16).astype(F32)
    along = jnp.sum(da * h1, -1, keepdims=True)
    dwide = da * scale1 - h1 * (scale1 * scale1 * scale1 * along * (1.0 / D))
    dh = (dy.astype(F32) + dwide.astype(BF16).astype(F32)).astype(BF16)
    dh_ref[...] = dh.T
    for j in range(FF // FC):
        at = slice(j * FC, (j + 1) * FC)
        _, dg, du = back(dot(dh, wd[0, at, :], nt), keep_g[:, at], keep_u[:, at])
        dg0[:, at], du0[:, at] = dg.astype(BF16), du.astype(BF16)


def tokens(x, dy, wg, wu, wd):
    n = x.shape[0]
    narrow = pl.BlockSpec((TT, D), lambda t: (t, 0))
    turned = pl.BlockSpec((D, TT), lambda t: (0, t))
    wide = pl.BlockSpec((TT, FF), lambda t: (t, 0))
    anywhere = pl.BlockSpec(memory_space=pl.ANY)
    big = jax.ShapeDtypeStruct((n, FF), BF16)
    return pl.pallas_call(
        tokens_kernel,
        grid=(n // TT,),
        in_specs=[narrow, narrow, anywhere, anywhere, anywhere],
        out_specs=[turned] * 4 + [wide] * 6,
        out_shape=[jax.ShapeDtypeStruct((D, n), BF16)] * 4 + [big] * 6,
        scratch_shapes=[
            pltpu.VMEM((2, D, FF), BF16),
            pltpu.VMEM((2, D, FF), BF16),
            pltpu.VMEM((2, FF, D), BF16),
            pltpu.VMEM((TT, FF), F32),
            pltpu.VMEM((TT, FF), F32),
            pltpu.SemaphoreType.DMA((6,)),
        ],
        compiler_params=pltpu.CompilerParams(dimension_semantics=("arbitrary",), vmem_limit_bytes=VMEM_LIMIT),
        name="tokens",
    )(x, dy, wg, wu, wd)


def part(ref, row, rows, block=0, blocks=ZS):
    return ref.at[pl.ds(pl.multiple_of(row, 16), rows), pl.ds(pl.multiple_of(block * D, D), blocks * D)]


def hold(rows, blocks=ZS):
    return pltpu.VMEM((rows, blocks * D), BF16)


def slabs(rows, blocks, body):
    n = rows // 16
    lax.fori_loop(0, n * blocks, lambda i, _: (body(lax.rem(i, n) * 16, i // n), 0)[1], 0)


def group_sum_kernel(layers_of, slots, smalls_key, *refs):
    count = len(slots)
    smalls, bigs, refs = refs[:count], refs[count : 2 * count], refs[2 * count :]
    outs, norm_out, refs = refs[:3], refs[3], refs[4:]
    own, r0, r1, r2, r3, r4, fin, refs = *(refs[i * count : (i + 1) * count] for i in range(7)), refs[7 * count :]
    square, told, send, recv, local, norm_send, norm_recv, staged, small, block, load_sem = refs
    full = [outs[slots[n]].at[layers_of[n]] for n in range(count)]

    i = lax.axis_index("dp")
    c, z, y, x = lax.rem(i, 2), lax.rem(i // 2, 4), lax.rem(i // 8, 2), i // 16

    def device(x, y, z, c):
        return {"dp": ((x * 2 + y) * 4 + z) * 2 + c}

    partner = device(x, y, z, 1 - c)
    by_x, by_y = device(1 - x, y, z, c), device(x, 1 - y, z, c)
    z0, z1 = lax.rem(z, 2), z // 2
    by_z0, by_z1 = device(x, y, z + 1 - 2 * z0, c), device(x, y, lax.rem(z + 2, 4), c)
    halves = ((x, z0, y, z1), (y, z0, x, z1))
    others = ((by_x, by_z0, by_y, by_z1), (by_y, by_z0, by_x, by_z1))

    def remote(n, slot, src, dst, to):
        return pltpu.make_async_remote_copy(
            src_ref=src, dst_ref=dst, send_sem=send.at[n, slot], recv_sem=recv.at[n, slot], device_id=to, device_id_type=MESH
        )

    def row_of(k, depth):
        f, g = halves[k][:2]
        return k * COLOR + (f * FIRST if depth >= 1 else 0) + (g * SECOND if depth >= 2 else 0)

    def small_load(n):
        return pltpu.make_async_copy(smalls[n], small.at[small_slot[n]], load_sem.at[2 + small_slot[n]])

    small_slot, new_small = [0], [True]
    for n in range(1, count):
        new_small.append(smalls_key[n] != smalls_key[n - 1])
        small_slot.append(small_slot[-1] ^ new_small[-1])

    def block_load(n, j, slot):
        at = pl.ds(pl.multiple_of(j * WIDE, WIDE), WIDE)
        return pltpu.make_async_copy(bigs[n].at[:, at], block.at[slot], load_sem.at[slot])

    def compute(n, mine):
        into = own[n] if mine else staged[n % 2]
        follows = n + mine
        if not mine:
            if new_small[n]:
                small_load(n).wait()
            if n >= 2:
                state0[n - 2].wait_send()
        turns = FF // WIDE // 2

        def body(p, _):
            for slot in range(2):
                j = 2 * p + slot
                block_load(n, j, slot).wait()
                for q in range(0, HALF, TALL):
                    rows = pl.ds(pl.multiple_of((c if mine else 1 - c) * HALF + q, TALL), TALL)
                    columns = pl.ds(pl.multiple_of(j * WIDE, WIDE), WIDE)
                    into[q : q + TALL, columns] = dot(small[small_slot[n], rows], block[slot]).astype(BF16)

                @pl.when(p < turns - 1)
                def _():
                    block_load(n, j + 2, slot).start()

                if follows < count:

                    @pl.when(p == turns - 1)
                    def _():
                        block_load(follows, slot, slot).start()

            return 0

        lax.fori_loop(0, turns, body, 0)
        if not mine and n + 1 < count and new_small[n + 1]:
            small_load(n + 1).start()

    state0 = {}

    def start0(n):
        theirs = remote(n, 0, staged[n % 2], r0[n], partner)
        theirs.start()
        state0[n] = theirs
        return [], [theirs]

    def at16(ref, row, b):
        return ref.at[pl.ds(pl.multiple_of(row, 16), 16), pl.ds(pl.multiple_of(b * D, D), D)]

    def partial(n, k, row, b, depth):
        s = halves[k][2]
        terms = [(own, row, b), (r0, row, b)]
        if depth >= 1:
            terms.append((r1, row - row_of(k, 1) + k * FIRST, b))
        if depth >= 2:
            terms.append((r2, row - row_of(k, 2) + k * SECOND, b))
        if depth >= 3:
            terms.append((r3, row - row_of(k, 2) + k * SECOND, b - 2 * s))
        if depth >= 4:
            terms.append((r4, row - row_of(k, 2) + k * SECOND, 0))
        value = None
        for ref, at, block_ in terms:
            term = at16(ref[n], at, block_)[...].astype(F32)
            value = term if value is None else value + term
        return value

    def send_half(step):
        def start(n):
            out = []
            for k in range(2):
                f, g, s, q = halves[k]
                if step == 1:
                    row, rows, b, blocks, into, to_row = k * COLOR + (1 - f) * FIRST, FIRST, 0, ZS, r1, k * FIRST
                elif step == 2:
                    row, rows, b, blocks, into, to_row = row_of(k, 1) + (1 - g) * SECOND, SECOND, 0, ZS, r2, k * SECOND
                elif step == 3:
                    row, rows, b, blocks, into, to_row = row_of(k, 2), SECOND, 2 * (1 - s), 2, r3, k * SECOND
                else:
                    row, rows, b, blocks, into, to_row = row_of(k, 2), SECOND, 2 * s + 1 - q, 1, r4, k * SECOND

                def body(r, bb):
                    at16(own[n], row + r, b + bb)[...] = partial(n, k, row + r, b + bb, step - 1).astype(BF16)

                slabs(rows, blocks, body)
                src = part(own[n], row, rows, b, blocks)
                out.append(remote(n, 2 * step - 1 + k, src, part(into[n], to_row, rows, 0, blocks), others[k][step - 1]))
                out[-1].start()
            return [], out

        return start

    def place(n, k, depth):
        f, g, s, q = halves[k]
        row, rows = (row_of(k, 2), SECOND) if depth >= 2 else (row_of(k, 1), FIRST)
        b, blocks = {4: (2 * s + q, 1), 3: (2 * s, 2)}.get(depth, (0, ZS))
        return part(full[n], c * HALF + row, rows, b, blocks)

    def finish(n):
        here, out = [], []
        for k in range(2):
            f, g, s, q = halves[k]

            def body(r, _):
                value = partial(n, k, row_of(k, 2) + r, 2 * s + q, 4).astype(BF16)
                at16(fin[n], k * SECOND + r, 0)[...] = value
                value = value.astype(F32)
                value = value * value
                pieces = [value[8 * a : 8 * a + 8, 128 * b : 128 * b + 128] for a in range(2) for b in range(D // 128)]
                square[...] += sum(pieces[1:], pieces[0])

            slabs(SECOND, 1, body)
            src = part(fin[n], k * SECOND, SECOND, 0, 1)
            here.append(pltpu.make_async_copy(src, place(n, k, 4), local.at[n, k]))
            here[-1].start()
            out.append(remote(n, 9 + k, src, place(n, k, 4), others[k][3]))
            out[-1].start()
        return here, out

    def pass_on(step):
        def start(n):
            out = []
            for k in range(2):
                where = place(n, k, step)
                out.append(remote(n, 17 - 2 * step + k, where, where, others[k][step - 1]))
                out[-1].start()
            return [], out

        return start

    def last(n):
        where = part(full[n], c * HALF, HALF)
        out = remote(n, 17, where, where, partner)
        out.start()
        return [], [out]

    stages = (start0, *(send_half(s) for s in (1, 2, 3, 4)), finish, *(pass_on(s) for s in (3, 2, 1)), last)
    state, sent = {}, []

    def run(n, stage):
        if stage:
            here, out = state[n]
            for copy in here:
                copy.wait()
            for copy in out:
                copy.wait_recv()
        if stage < len(stages):
            state[n] = stages[stage](n)
            if stage:
                sent.extend(state[n][1])

    square[...] = jnp.zeros_like(square)
    small_load(0).start()
    for which in range(2):
        block_load(0, which, which).start()
    exchange = [partner, by_x, by_y, by_z0, by_z1]
    norm_step, pending = 0, None

    def norm_round():
        nonlocal norm_step, pending
        if pending is not None:
            pending.wait()
            told[2 * norm_step + 2] = told[2 * norm_step] + told[2 * norm_step + 1]
            norm_step += 1
            pending = None
        if norm_step < len(exchange):
            pending = pltpu.make_async_remote_copy(
                src_ref=told.at[2 * norm_step],
                dst_ref=told.at[2 * norm_step + 1],
                send_sem=norm_send.at[norm_step],
                recv_sem=norm_recv.at[norm_step],
                device_id=exchange[norm_step],
                device_id_type=MESH,
            )
            pending.start()

    halves_done = finished = 0
    for n, stage in ORDER:
        if stage is None:
            compute(halves_done // 2, halves_done % 2)
            if halves_done % 2 == 0:
                run(halves_done // 2, 0)
            halves_done += 1
            continue
        run(n, stage)
        finished += stage == 5
        if finished == count:
            if stage == 5:
                told[0] = square[...]
            norm_round()
    while norm_step < len(exchange):
        norm_round()
    norm_out[...] = told[2 * len(exchange)]
    for n in range(count):
        run(n, len(stages))
    for copy in sent + [state0[n] for n in range(count - 2, count)]:
        copy.wait_send()


ORDER = (
    (None, None), (None, None), (0, 1), (None, None), (None, None), (0, 2), (1, 1), (None, None), (None, None), (0, 3),
    (1, 2), (2, 1), (None, None), (0, 4), (None, None), (0, 5), (1, 3), (2, 2), (3, 1), (None, None),
    (1, 4), (0, 6), (None, None), (2, 3), (3, 2), (1, 5), (4, 1), (0, 7), (None, None), (2, 4),
    (None, None), (3, 3), (4, 2), (5, 1), (1, 6), (3, 4), (2, 5), (5, 2), (1, 7), (4, 3),
    (3, 5), (4, 4), (2, 6), (2, 7), (5, 3), (0, 8), (5, 4), (1, 8), (3, 6), (4, 5),
    (0, 9), (1, 9), (2, 8), (5, 5), (3, 7), (4, 6), (5, 6), (2, 9), (4, 7), (5, 7),
    (3, 8), (4, 8), (3, 9), (5, 8), (4, 9), (5, 9),
)


def group_sum(pairs, layers_of, slots, smalls_key):
    count = len(pairs)
    scratch = []
    for one in (
        hold(HALF),
        hold(HALF),
        hold(2 * FIRST),
        hold(2 * SECOND),
        hold(2 * SECOND, 2),
        hold(2 * SECOND, 1),
        hold(2 * SECOND, 1),
    ):
        scratch += [one] * count
    dma = pltpu.SemaphoreType.DMA
    scratch += [
        pltpu.VMEM((8, 128), F32),
        pltpu.VMEM((11, 8, 128), F32),
        dma((count, 18)),
        dma((count, 18)),
        dma((count, 2)),
        dma((5,)),
        dma((5,)),
        [hold(HALF)] * 2,
        pltpu.VMEM((2, *pairs[0][0].shape), BF16),
        pltpu.VMEM((2, pairs[0][1].shape[0], WIDE), BF16),
        dma((4,)),
    ]
    out = pl.pallas_call(
        functools.partial(group_sum_kernel, layers_of, slots, smalls_key),
        out_shape=(
            jax.ShapeDtypeStruct((2, D, FF), BF16),
            jax.ShapeDtypeStruct((2, D, FF), BF16),
            jax.ShapeDtypeStruct((2, D, FF), BF16),
            jax.ShapeDtypeStruct((8, 128), F32),
        ),
        in_specs=[pl.BlockSpec(memory_space=pl.ANY)] * (2 * count),
        out_specs=(pl.BlockSpec(memory_space=pl.ANY),) * 3 + (pl.BlockSpec(memory_space=pltpu.VMEM),),
        scratch_shapes=scratch,
        compiler_params=pltpu.CompilerParams(has_side_effects=True, vmem_limit_bytes=VMEM_LIMIT),
        name="group_sum",
    )(*[small for small, _ in pairs], *[big for _, big in pairs])
    return out


def solution(mesh):
    def step(x, dy, *arrays):
        weights, m, v = (arrays[i : i + 3] for i in (0, 3, 6))
        a0, a1, dy_t, dh_t, act0, dg0, du0, act1, dg1, du1 = tokens(x[0], dy[0], *weights)
        pairs = ((dy_t, act1), (a1, dg1), (a1, du1), (dh_t, act0), (a0, dg0), (a0, du0))
        *summed, square = group_sum(pairs, (1, 1, 1, 0, 0, 0), (2, 0, 1) * 2, (0, 1, 1, 2, 3, 3))
        flat = [one.reshape(-1, one.shape[-1]) for one in (*weights, *m, *v, *summed)]
        return tuple(one.reshape(weights[k % 3].shape) for k, one in enumerate(adamw(square, *flat)))

    return jax.shard_map(
        step,
        mesh=mesh,
        in_specs=(P(("rep", "dp"), None, None),) * 2 + (P(None, None, None),) * 9,
        out_specs=(P("rep", None, None),) * 9,
        check_vma=False,
    )
```

time: 897 us -> 502 us (0.56)
  Pallas kernels: 0 us -> 501 us
  waiting for transfers between devices: 433 us -> 0 us
  matrix products: 299 us -> 0 us
  other arithmetic: 131 us -> 0 us
  between operations: 16.7 us -> 0.83 us
  local copies, waits for them, and re-layouts: 9.95 us -> 0 us
    pallas_call x0 -> x3, Pallas kernels: none -> 501 us  [the longest x1 268 us: group_sum(): pl.pallas_call(functools.partial(group_sum_kernel, layers_of, slots, smal...]
    psum x1 -> x0, waiting for transfers between devices: 433 us -> none  [step(): summed[number] = [lax.psum(by_w[name], 'dp') for name in NAMES]]
    dot_general x15 -> x0, matrix products: 299 us -> none  [the longest x5 115 us: layer(): gate = jnp.dot(a, w['w_gate'], preferred_element_type=jnp.float32)]
    convert_element_type x2 -> x0, other arithmetic: 100 us -> none  [adamw(): return ((w - 0.02 * step).astype(jnp.bfloat16), m, v)]
    reduce_sum x4 -> x0, other arithmetic: 24.8 us -> none  [the longest x3 24.1 us: step(): jnp.sum(g * g)]
    unnamed x40 -> x0, local copies, waits for them, and re-layouts: 9.95 us -> none
  transfers between devices with their start and end apart: 1 -> 0, of which waited for: 1 -> 0; matrix products, arithmetic and copies ran while one was open for 0% -> 0% of each run, Pallas kernels for 0% -> 0%
where the time goes in v1:
time: 502 us; the launch traced here: 501 us
  Pallas kernels  501 us (100%)
    pallas_call x1, Pallas kernels, group_sum(): pl.pallas_call(functools.partial(group_sum_kernel, layers_of, slots, smal...  268 us
    pallas_call x1, Pallas kernels, tokens(): pl.pallas_call(tokens_kernel, grid=(n // TT,), in_specs=[narrow, narrow,...  117 us
    pallas_call x1, Pallas kernels, adamw(): pl.pallas_call(functools.partial(adamw_kernel, sum((w.size for w in array...  116 us

profile of v1, /device:TPU:0, one launch (start us, length us, event | category | flops | bytes accessed | tf_op | source)
XLA Modules:
  0.0 501.5 jit_solution(3288287383672694660)
XLA Ops:
  0.6 117.1 %tokens.1 = (bf16[768,2048]{1,0:T(8,128)(2,1)}, bf16[768,2048]{1,0:T(8,128)(2,1)}, bf16[768,2048]{1,0:T(8,128)(2,1)}, bf16[768,2048]{1,0:T(8,128)(2,1)}, bf16[20...) custom-call(bf16[2048,768]{1,0:T(8,128)(2,1)} %bitcast.35, ...), custom_call_target="tpu_custom_call" | custom-call | tf_op jit(solution)/shard_map/tokens/pallas_call | solution.py:149
  117.7 267.9 %group_sum.1 = (bf16[2,768,3072]{2,1,0:T(8,128)(2,1)}, bf16[2,768,3072]{2,1,0:T(8,128)(2,1)}, bf16[2,768,3072]{2,1,0:T(8,128)(2,1)}, f32[8,128]{1,0:T(8,128)}) custom-call(bf16[768,2048]{1,0:T(8,128)(2,1)} %get-tuple-element.32.refs_0_, bf16[768,2048]{1,0:T(8,128)(2,1)} %get-tuple-element.33.refs_1_.refs_2_, ...), custom_call_target="tpu_custom_call" | custom-call | tf_op jit(solution)/shard_map/group_sum/pallas_call | solution.py:456
  385.6 115.6 %adamw.1 = (bf16[1536,3072]{1,0:T(8,128)(2,1)}, bf16[1536,3072]{1,0:T(8,128)(2,1)}, bf16[6144,768]{1,0:T(8,128)(2,1)}, f32[1536,3072]{1,0:T(8,128)}, f32[1536,30...) custom-call(f32[8,128]{1,0:T(8,128)} %get-tuple-element.42.square_ref, ...), custom_call_target="tpu_custom_call" | custom-call | tf_op jit(solution)/shard_map/adamw/pallas_call | solution.py:54
